TPU v7x, 256 devices: a whole 4x4x8 slice. The times are simulated.
256 devices in a mesh: segment: 4 (over y), vocab: 64 (over z, x, core).
Axes of the slice: x: 4, y: 4, z: 8, core: 2. Of those that a mesh axis runs over, the one named last changes fastest.
Arguments:
- trunk_out: bfloat16 [160, 7168], P(None, 'vocab'), may hold values from -12 to 12
- embeds: bfloat16 [164, 7168], P(None, 'vocab'), may hold values from -12 to 12
- token_ids: int32 [164], replicated, may hold values from 0 to 65535
- module_weight: bfloat16 [4, 2, 7168, 7168], P('segment', None, 'vocab'), may hold values from -0.046875 to 0.046875
- hidden_gain: bfloat16 [3, 7168], P(None, 'vocab'), may hold values from 0.25 to 1.75
- embed_gain: bfloat16 [3, 7168], P(None, 'vocab'), may hold values from 0.25 to 1.75
- out_gain: bfloat16 [4, 7168], P('segment'), may hold values from 0.25 to 1.75
- head_weight: bfloat16 [7168, 65536], P('segment', 'vocab'), may hold values from -0.21260502 to 0.21260502
Outputs:
- losses: float32 [4, 160], P('segment')
All inputs are finite; a program needn't handle non-finite values.
Results may differ from a plain program's by a relative error of at most 0.00095.
Values may be sent and summed in bfloat16 or wider, within the bound.
A program may use at most 128 MiB of HBM per device.

v0:
```python
import jax
import jax.numpy as jnp
from jax import lax
from jax.sharding import PartitionSpec as P

D = 7168
TOK = 160
MICRO = 4


EPSILON = 1e-06


def copy_for_each(shard, axis):
    copies = jnp.broadcast_to(shard, (lax.axis_size(axis), *shard.shape))
    return lax.all_to_all(copies, axis, split_axis=0, concat_axis=0, tiled=True)


def over_copies(shard, axis):
    return copy_for_each(shard, axis).sum(axis=0)


def cut_along(shard, dim, count):
    before, after = (shard.shape[:dim], shard.shape[dim + 1 :])
    return jnp.moveaxis(shard.reshape(*before, count, -1, *after), dim, 0)


def summed_on_arrival(shard, axis, dim):
    count = lax.axis_size(axis)
    blocks = lax.all_to_all(cut_along(shard, dim, count), axis, 0, 0, tiled=True)
    return jnp.sum(blocks, axis=0)


def in_order(blocks, dim):
    dims = list(blocks.shape[1:])
    dims[dim] *= blocks.shape[0]
    return jnp.moveaxis(blocks, 0, dim).reshape(dims)


def collect(shard, axis, dim):
    blocks = copy_for_each(shard, axis)
    return in_order(blocks, dim)


def passed_along(block, axis, distance):
    devices = range(lax.axis_size(axis))
    route = [(i - distance, i) for i in devices if i - distance in devices]
    return lax.ppermute(block, axis, route)


def collected_together(shard, axis):
    leaves = jax.tree.leaves(shard)
    order = sorted(range(len(leaves)), key=lambda k: -leaves[k].size)
    width = (1, *leaves[order[0]].shape)[-1]
    lines = [
        jnp.pad(leaves[k].reshape(-1), (0, -leaves[k].size % width)).reshape(-1, width)
        for k in order
    ]
    both, at, found = (copy_for_each(jnp.concatenate(lines), axis), 0, {})
    for k, line in zip(order, lines):
        share = both[:, at : at + len(line)].reshape(len(both), -1)
        found[k] = share[:, : leaves[k].size].reshape(-1, *leaves[k].shape)
        at += len(line)
    numbers = iter(range(len(leaves)))
    return jax.tree.map(lambda _: found[next(numbers)], shard)


def combined_pairwise(pieces, combine):
    while len(jax.tree.leaves(pieces)[0]) > 1:
        pieces = jax.vmap(combine)(
            *(jax.tree.map(lambda part: part[side::2], pieces) for side in (0, 1))
        )
    return jax.tree.map(lambda part: part[0], pieces)


def joined_all(shard, axis, combine):
    pieces = collected_together(shard, axis)
    return combined_pairwise(pieces, combine)


def merge_softmax(earlier, second):
    highest = jnp.maximum(earlier[0], second[0])
    summed = earlier[1] * jnp.exp(earlier[0] - highest) + second[1] * jnp.exp(second[0] - highest)
    return (highest, summed, earlier[2] + second[2])


def per_device(
    trunk_out, embeds, token_ids, module_weight, hidden_gain, embed_gain, out_gain, head_weight
):
    sections = lax.axis_size("segment")
    section = lax.axis_index("segment")
    shard_index = lax.axis_index("vocab")
    local_width = trunk_out.shape[1]
    micro_rows = TOK // MICRO
    vocab_width = head_weight.shape[1]
    depth_count = hidden_gain.shape[0]
    embed_float = embeds.astype(jnp.float32)
    embed_squares = over_copies(jnp.sum(embed_float * embed_float, axis=1), "vocab")
    embed_scale = lax.rsqrt(embed_squares / D + EPSILON)
    module_index = jnp.maximum(section - 1, 0)
    module_block = module_weight[0]
    embed_scaling = lax.dynamic_index_in_dim(embed_gain, module_index, 0, keepdims=False).astype(
        jnp.float32
    )
    next_scaling = lax.dynamic_index_in_dim(
        hidden_gain, jnp.minimum(section, depth_count - 1), 0, keepdims=False
    ).astype(jnp.float32)
    out_scaling = out_gain[0].astype(jnp.float32)
    targets = lax.dynamic_slice_in_dim(token_ids, section + 1, TOK, 0) - shard_index * vocab_width
    whole_head = lax.all_gather(head_weight, "segment", axis=0, tiled=True)
    column_ids = lax.broadcasted_iota(jnp.int32, (micro_rows, vocab_width), 1)
    incoming = jnp.zeros((micro_rows, local_width), jnp.bfloat16)
    stored_tops = jnp.zeros((TOK,), jnp.float32)
    stored_totals = jnp.ones((TOK,), jnp.float32)
    stored_picks = jnp.zeros((TOK,), jnp.float32)
    for moment in range(MICRO + sections - 1):
        micro_index = moment - section
        active = (micro_index >= 0) & (micro_index < MICRO)
        first_row = jnp.clip(micro_index, 0, MICRO - 1) * micro_rows
        own_rows = lax.dynamic_slice_in_dim(trunk_out, first_row, micro_rows, 0)
        embed_rows = lax.dynamic_slice_in_dim(embed_float, first_row + section, micro_rows, 0)
        embed_factor = lax.dynamic_slice_in_dim(embed_scale, first_row + section, micro_rows, 0)
        embed_normed = (embed_rows * embed_factor[:, None] * embed_scaling).astype(jnp.bfloat16)
        partial_value = jnp.dot(incoming, module_block[0], preferred_element_type=jnp.float32)
        partial_value = partial_value + jnp.dot(
            embed_normed, module_block[1], preferred_element_type=jnp.float32
        )
        leading = section == 0
        columns = summed_on_arrival(partial_value, "vocab", 1).astype(jnp.bfloat16)
        columns = jnp.where(leading, own_rows, columns)
        full_rows = collect(columns, "vocab", 1)
        rows_float = full_rows.astype(jnp.float32)
        inverse_rms = lax.rsqrt(jnp.mean(rows_float * rows_float, axis=1, keepdims=True) + EPSILON)
        head_input = (rows_float * inverse_rms * out_scaling).astype(jnp.bfloat16)
        own_columns = lax.dynamic_slice_in_dim(
            rows_float, shard_index * local_width, local_width, 1
        )
        passed = (own_columns * inverse_rms * next_scaling).astype(jnp.bfloat16)
        incoming = passed_along(passed, "segment", 1)
        logits = jnp.dot(head_input, whole_head, preferred_element_type=jnp.float32)
        row_targets = lax.dynamic_slice_in_dim(targets, first_row, micro_rows, 0)
        row_target = jnp.sum(jnp.where(column_ids == row_targets[:, None], logits, 0.0), axis=1)
        row_top = jnp.max(logits, axis=1)
        row_total = jnp.sum(jnp.exp(logits - row_top[:, None]), axis=1)
        stored_tops = jnp.where(
            active, lax.dynamic_update_slice_in_dim(stored_tops, row_top, first_row, 0), stored_tops
        )
        stored_totals = jnp.where(
            active,
            lax.dynamic_update_slice_in_dim(stored_totals, row_total, first_row, 0),
            stored_totals,
        )
        stored_picks = jnp.where(
            active,
            lax.dynamic_update_slice_in_dim(stored_picks, row_target, first_row, 0),
            stored_picks,
        )
    merged_tops, merged_totals, merged_picks = joined_all(
        (stored_tops, stored_totals, stored_picks), "vocab", merge_softmax
    )
    losses = merged_tops + jnp.log(merged_totals) - merged_picks
    return losses[None, :]


def solution(mesh):
    in_specs = (
        P(None, "vocab"),
        P(None, "vocab"),
        P(),
        P("segment", None, "vocab", None),
        P(None, "vocab"),
        P(None, "vocab"),
        P("segment", None),
        P("segment", "vocab"),
    )
    out_specs = P("segment", None)
    return jax.shard_map(
        per_device, mesh=mesh, in_specs=in_specs, out_specs=out_specs, check_vma=False
    )
```

profile of v0, /device:TPU:1, one launch (start us, length us, event | category | flops | bytes accessed | tf_op | source)
XLA Modules:
  0.0 680.7 jit_solution(8780931611484874384)
XLA Ops:
  8.1 13.2 %all-to-all-start = ((f32[64,1,164]{2,1,0:T(1,128)}), f32[64,1,164]{2,1,0:T(1,128)S(1)}, u32[]{:S(2)}, u32[]{:S(2)}) async-start(f32[64,1,164]{2,1,0:T(1,128)} %broadcast_in_dim.33), calls=%async_computation | async-start | bytes 131072 | tf_op jit(solution)/shard_map/all_to_all | solution.py:16
  22.2 2.8 fusion.19
  25.0 6.5 all-to-all-done
  31.6 2.7 convolution_add_fusion.6
  34.3 3.1 reshape.157
  37.4 3.2 copy.78
  40.5 5.3 all-to-all-start.1
  45.8 33.7 %all-to-all-done.1 = f32[64,40,112]{2,1,0:T(8,128)} async-done(((f32[64,40,112]{2,1,0:T(8,128)}), f32[64,40,112]{2,1,0:T(8,128)}, u32[]{:S(2)}, u32[]{:S(2)}) %all-to-all-start.1) | async-done | bytes 1146912 | tf_op jit(solution)/shard_map/all_to_all | solution.py:30
  79.6 1.4 reduce_sum.272
  82.0 6.5 all-to-all-start.2
  88.5 20.2 %all-to-all-done.2 = bf16[64,40,112]{2,1,0:T(8,128)(2,1)} async-done(((bf16[64,40,112]{2,1,0:T(8,128)(2,1)}), bf16[64,40,112]{2,1,0:T(8,128)(2,1)}, u32[]{:S(2)}, u32[]{:S(2)}) %all-to-all-start.2) | async-done | bytes 573472 | tf_op jit(solution)/shard_map/all_to_all | solution.py:16
  111.2 3.2 reshape.174
  116.7 3.2 collective-permute-start
  122.0 3.1 reshape.158
  125.1 3.2 copy.77
  128.2 6.8 %all-to-all-start.3 = ((f32[64,40,112]{2,1,0:T(8,128)}), f32[64,40,112]{2,1,0:T(8,128)}, u32[]{:S(2)}, u32[]{:S(2)}) async-start(f32[64,40,112]{2,1,0:T(8,128)} %bitcast.116), calls=%async_computation.3 | async-start | bytes 2621440 | tf_op jit(solution)/shard_map/all_to_all | solution.py:30
  135.1 33.6 %all-to-all-done.3 = f32[64,40,112]{2,1,0:T(8,128)} async-done(((f32[64,40,112]{2,1,0:T(8,128)}), f32[64,40,112]{2,1,0:T(8,128)}, u32[]{:S(2)}, u32[]{:S(2)}) %all-to-all-start.3) | async-done | bytes 1146912 | tf_op jit(solution)/shard_map/all_to_all | solution.py:30
  171.0 6.5 all-to-all-start.4
  178.3 19.5 %all-to-all-done.4 = bf16[64,40,112]{2,1,0:T(8,128)(2,1)} async-done(((bf16[64,40,112]{2,1,0:T(8,128)(2,1)}), bf16[64,40,112]{2,1,0:T(8,128)(2,1)}, u32[]{:S(2)}, u32[]{:S(2)}) %all-to-all-start.4) | async-done | bytes 573472 | tf_op jit(solution)/shard_map/all_to_all | solution.py:16
  200.4 3.3 reshape.177
  206.0 3.9 collective-permute-start.1
  212.2 3.1 reshape.159
  215.3 3.2 copy.76
  218.5 6.9 %all-to-all-start.5 = ((f32[64,40,112]{2,1,0:T(8,128)}), f32[64,40,112]{2,1,0:T(8,128)}, u32[]{:S(2)}, u32[]{:S(2)}) async-start(f32[64,40,112]{2,1,0:T(8,128)} %bitcast.117), calls=%async_computation.5 | async-start | bytes 2621440 | tf_op jit(solution)/shard_map/all_to_all | solution.py:30
  225.4 33.6 %all-to-all-done.5 = f32[64,40,112]{2,1,0:T(8,128)} async-done(((f32[64,40,112]{2,1,0:T(8,128)}), f32[64,40,112]{2,1,0:T(8,128)}, u32[]{:S(2)}, u32[]{:S(2)}) %all-to-all-start.5) | async-done | bytes 1146912 | tf_op jit(solution)/shard_map/all_to_all | solution.py:30
  260.5 26.5 %all_to_all.81 = bf16[64,40,112]{2,1,0:T(8,128)(2,1)S(1)} all-to-all(bf16[64,40,112]{2,1,0:T(8,128)(2,1)S(1)} %broadcast_in_dim.36), channel_id=1, replica_groups=mesh['segment'=4,'vocab'=64] {'vocab'}, dimensions={0} | all-to-all | bytes 1146880 | tf_op jit(solution)/shard_map/all_to_all | solution.py:16
  289.2 3.2 reshape.178
  294.7 4.1 collective-permute-start.2
  301.1 3.1 reshape.160
  304.2 3.1 copy.75
  307.3 6.8 %all-to-all-start.7 = ((f32[64,40,112]{2,1,0:T(8,128)}), f32[64,40,112]{2,1,0:T(8,128)}, u32[]{:S(2)}, u32[]{:S(2)}) async-start(f32[64,40,112]{2,1,0:T(8,128)} %bitcast.118), calls=%async_computation.7 | async-start | bytes 2621440 | tf_op jit(solution)/shard_map/all_to_all | solution.py:30
  314.1 33.6 %all-to-all-done.7 = f32[64,40,112]{2,1,0:T(8,128)} async-done(((f32[64,40,112]{2,1,0:T(8,128)}), f32[64,40,112]{2,1,0:T(8,128)}, u32[]{:S(2)}, u32[]{:S(2)}) %all-to-all-start.7) | async-done | bytes 1146912 | tf_op jit(solution)/shard_map/all_to_all | solution.py:30
  349.3 26.9 %all_to_all.82 = bf16[64,40,112]{2,1,0:T(8,128)(2,1)S(1)} all-to-all(bf16[64,40,112]{2,1,0:T(8,128)(2,1)S(1)} %broadcast_in_dim.37), channel_id=1, replica_groups=mesh['segment'=4,'vocab'=64] {'vocab'}, dimensions={0} | all-to-all | bytes 1146880 | tf_op jit(solution)/shard_map/all_to_all | solution.py:16
  378.4 3.2 reshape.179
  383.9 4.1 collective-permute-start.3
  390.1 3.1 reshape.161
  393.2 3.1 copy.74
  396.3 6.8 %all-to-all-start.9 = ((f32[64,40,112]{2,1,0:T(8,128)}), f32[64,40,112]{2,1,0:T(8,128)}, u32[]{:S(2)}, u32[]{:S(2)}) async-start(f32[64,40,112]{2,1,0:T(8,128)} %bitcast.119), calls=%async_computation.9 | async-start | bytes 2621440 | tf_op jit(solution)/shard_map/all_to_all | solution.py:30
  403.2 33.6 %all-to-all-done.9 = f32[64,40,112]{2,1,0:T(8,128)} async-done(((f32[64,40,112]{2,1,0:T(8,128)}), f32[64,40,112]{2,1,0:T(8,128)}, u32[]{:S(2)}, u32[]{:S(2)}) %all-to-all-start.9) | async-done | bytes 1146912 | tf_op jit(solution)/shard_map/all_to_all | solution.py:30
  438.3 26.5 %all_to_all.83 = bf16[64,40,112]{2,1,0:T(8,128)(2,1)S(1)} all-to-all(bf16[64,40,112]{2,1,0:T(8,128)(2,1)S(1)} %broadcast_in_dim.38), channel_id=1, replica_groups=mesh['segment'=4,'vocab'=64] {'vocab'}, dimensions={0} | all-to-all | bytes 1146880 | tf_op jit(solution)/shard_map/all_to_all | solution.py:16
  467.0 3.2 reshape.180
  472.5 3.9 collective-permute-start.4
  478.6 3.1 reshape.162
  481.7 3.1 copy.73
  484.8 6.8 %all-to-all-start.11 = ((f32[64,40,112]{2,1,0:T(8,128)}), f32[64,40,112]{2,1,0:T(8,128)}, u32[]{:S(2)}, u32[]{:S(2)}) async-start(f32[64,40,112]{2,1,0:T(8,128)} %bitcast.120), calls=%async_computation.11 | async-start | bytes 2621440 | tf_op jit(solution)/shard_map/all_to_all | solution.py:30
  491.6 33.6 %all-to-all-done.11 = f32[64,40,112]{2,1,0:T(8,128)} async-done(((f32[64,40,112]{2,1,0:T(8,128)}), f32[64,40,112]{2,1,0:T(8,128)}, u32[]{:S(2)}, u32[]{:S(2)}) %all-to-all-start.11) | async-done | bytes 1146912 | tf_op jit(solution)/shard_map/all_to_all | solution.py:30
  527.6 6.8 %all-to-all-start.12 = ((bf16[64,40,112]{2,1,0:T(8,128)(2,1)}), bf16[64,40,112]{2,1,0:T(8,128)(2,1)}, u32[]{:S(2)}, u32[]{:S(2)}) async-start(bf16[64,40,112]{2,1,0:T(8,128)(2,1)} %broadcast_in_dim.39), calls=%async_computation.12 | async-start | bytes 1310720 | tf_op jit(solution)/shard_map/all_to_all | solution.py:16
  534.8 19.8 %all-to-all-done.12 = bf16[64,40,112]{2,1,0:T(8,128)(2,1)} async-done(((bf16[64,40,112]{2,1,0:T(8,128)(2,1)}), bf16[64,40,112]{2,1,0:T(8,128)(2,1)}, u32[]{:S(2)}, u32[]{:S(2)}) %all-to-all-start.12) | async-done | bytes 573472 | tf_op jit(solution)/shard_map/all_to_all | solution.py:16
  557.0 3.2 reshape.181
  562.5 3.9 collective-permute-start.5
  568.6 2.0 reshape.164
  570.6 1.8 copy.72
  572.5 7.0 %all-to-all-start.13 = ((f32[64,40,112]{2,1,0:T(8,128)}), f32[64,40,112]{2,1,0:T(8,128)}, u32[]{:S(2)}, u32[]{:S(2)}) async-start(f32[64,40,112]{2,1,0:T(8,128)} %bitcast.114), calls=%async_computation.13 | async-start | bytes 2621440 | tf_op jit(solution)/shard_map/all_to_all | solution.py:30
  579.5 8.1 %fusion.117 = (f32[40]{0:T(128)S(1)}, f32[40,1024]{1,0:T(8,128)S(1)}) fusion(bf16[7168,1024]{1,0:T(8,128)(2,1)} %all-gather.2.cloned.1.call-done, f32[40,7168]{1,0:T(8,128)S(1)} %copy-done.2, f32[7168]{0:T(1024)S(1)} %bitcast.107, f32[40]{0:T(128)S(1)} %add_rsqrt_fusion.7), kind=kOutput, calls=%fused_computation.239 | convolution fusion | flops 588103616 | bytes 16019776 | tf_op jit(solution)/shard_map/dot_general | solution.py:140
  589.1 2.9 fusion.118
  592.6 2.9 fusion.120
  595.5 2.9 fusion.121
  598.6 2.9 fusion.119
  603.3 9.7 %all-to-all-done.13 = f32[64,40,112]{2,1,0:T(8,128)} async-done(((f32[64,40,112]{2,1,0:T(8,128)}), f32[64,40,112]{2,1,0:T(8,128)}, u32[]{:S(2)}, u32[]{:S(2)}) %all-to-all-start.13) | async-done | bytes 1146912 | tf_op jit(solution)/shard_map/all_to_all | solution.py:30
  615.4 6.3 all-to-all-start.14
  621.9 8.0 %fusion.122 = (f32[40]{0:T(128)S(1)}, f32[40,1024]{1,0:T(8,128)S(1)}) fusion(bf16[7168,1024]{1,0:T(8,128)(2,1)} %all-gather.2.cloned.1.call-done, f32[40,7168]{1,0:T(8,128)S(1)} %copy-done.7, f32[40]{0:T(128)S(1)} %add_rsqrt_fusion.2, f32[7168]{0:T(1024)S(1)} %bitcast.112), kind=kOutput, calls=%fused_computation.244 | convolution fusion | flops 588103616 | bytes 16019776 | tf_op jit(solution)/shard_map/dot_general | solution.py:140
  630.3 11.8 %all-to-all-done.14 = bf16[64,40,112]{2,1,0:T(8,128)(2,1)S(1)} async-done(((bf16[64,40,112]{2,1,0:T(8,128)(2,1)}), bf16[64,40,112]{2,1,0:T(8,128)(2,1)S(1)}, u32[]{:S(2)}, u32[]{:S(2)}) %all-to-all-start.14) | async-done | bytes 573472 | tf_op jit(solution)/shard_map/all_to_all | solution.py:16
  643.6 8.0 %fusion.123 = (f32[40]{0:T(128)S(1)}, f32[40,1024]{1,0:T(8,128)S(1)}) fusion(bf16[7168,1024]{1,0:T(8,128)(2,1)} %all-gather.2.cloned.1.call-done, f32[40,7168]{1,0:T(8,128)S(1)} %reshape.182, f32[40]{0:T(128)S(1)} %add_rsqrt_fusion.1, f32[7168]{0:T(1024)S(1)} %bitcast.113), kind=kOutput, calls=%fused_computation.245 | convolution fusion | flops 588103616 | bytes 16019776 | tf_op jit(solution)/shard_map/dot_general | solution.py:140
  653.5 16.7 %all_to_all.84 = f32[64,1,480]{2,1,0:T(1,128)S(1)} all-to-all(f32[64,1,480]{2,1,0:T(1,128)S(1)} %reshape.183), channel_id=1, replica_groups=mesh['segment'=4,'vocab'=64] {'vocab'}, dimensions={0} | all-to-all | bytes 245760 | tf_op jit(solution)/shard_map/all_to_all | solution.py:16
  (201 shorter events, 68.6 us)
Async XLA Ops:
  7.4 17.5 %copy-start.14 = (bf16[3,112]{1,0:T(4,128)(2,1)S(1)}, bf16[3,112]{1,0:T(4,128)(2,1)}, u32[]{:S(2)}) copy-start(bf16[3,112]{1,0:T(4,128)(2,1)} %param.13) | copy-start | bytes 2020
  8.1 23.5 %copy-start.1 = (bf16[1,2,112,7168]{3,2,1,0:T(8,128)(2,1)S(1)}, bf16[1,2,112,7168]{3,2,1,0:T(8,128)(2,1)}, u32[]{:S(2)}) copy-start(bf16[1,2,112,7168]{3,2,1,0:T(8,128)(2,1)} %param.11) | copy-start | bytes 9633796
  8.1 23.3 %all-to-all-start = ((f32[64,1,164]{2,1,0:T(1,128)}), f32[64,1,164]{2,1,0:T(1,128)S(1)}, u32[]{:S(2)}, u32[]{:S(2)}) async-start(f32[64,1,164]{2,1,0:T(1,128)} %broadcast_in_dim.33), calls=%async_computation | async-start | bytes 131072 | tf_op jit(solution)/shard_map/all_to_all | solution.py:16
  40.5 39.0 %all-to-all-start.1 = ((f32[64,40,112]{2,1,0:T(8,128)}), f32[64,40,112]{2,1,0:T(8,128)}, u32[]{:S(2)}, u32[]{:S(2)}) async-start(f32[64,40,112]{2,1,0:T(8,128)} %bitcast.115), calls=%async_computation.1 | async-start | bytes 2621440 | tf_op jit(solution)/shard_map/all_to_all | solution.py:30
  45.8 35.2 %copy-start.11 = (bf16[160,112]{1,0:T(8,128)(2,1)S(1)}, bf16[160,112]{1,0:T(8,128)(2,1)}, u32[]{:S(2)}) copy-start(bf16[160,112]{1,0:T(8,128)(2,1)} %param.8) | copy-start | bytes 107524
  81.0 7.4 %copy-start.15 = (bf16[3,112]{1,0:T(4,128)(2,1)S(1)}, bf16[3,112]{1,0:T(4,128)(2,1)}, u32[]{:S(2)}) copy-start(bf16[3,112]{1,0:T(4,128)(2,1)} %param.12) | copy-start | bytes 2020
  82.0 26.7 %all-to-all-start.2 = ((bf16[64,40,112]{2,1,0:T(8,128)(2,1)}), bf16[64,40,112]{2,1,0:T(8,128)(2,1)}, u32[]{:S(2)}, u32[]{:S(2)}) async-start(bf16[64,40,112]{2,1,0:T(8,128)(2,1)} %broadcast_in_dim.34), calls=%async_computation.2 | async-start | bytes 1310720 | tf_op jit(solution)/shard_map/all_to_all | solution.py:16
  116.7 4.0 collective-permute-start
  128.2 40.4 %all-to-all-start.3 = ((f32[64,40,112]{2,1,0:T(8,128)}), f32[64,40,112]{2,1,0:T(8,128)}, u32[]{:S(2)}, u32[]{:S(2)}) async-start(f32[64,40,112]{2,1,0:T(8,128)} %bitcast.116), calls=%async_computation.3 | async-start | bytes 2621440 | tf_op jit(solution)/shard_map/all_to_all | solution.py:30
  171.0 26.8 %all-to-all-start.4 = ((bf16[64,40,112]{2,1,0:T(8,128)(2,1)}), bf16[64,40,112]{2,1,0:T(8,128)(2,1)}, u32[]{:S(2)}, u32[]{:S(2)}) async-start(bf16[64,40,112]{2,1,0:T(8,128)(2,1)} %broadcast_in_dim.35), calls=%async_computation.4 | async-start | bytes 1310720 | tf_op jit(solution)/shard_map/all_to_all | solution.py:16
  177.5 401.9 %all-gather.2.cloned.1.call-start = ((), (), s32[]{:S(2)}) async-start(), calls=%async_computation.16 | async-start | bytes 18350080 | tf_op jit(solution)/shard_map/all_gather | solution.py:110
  206.0 4.9 collective-permute-start.1
  218.5 40.4 %all-to-all-start.5 = ((f32[64,40,112]{2,1,0:T(8,128)}), f32[64,40,112]{2,1,0:T(8,128)}, u32[]{:S(2)}, u32[]{:S(2)}) async-start(f32[64,40,112]{2,1,0:T(8,128)} %bitcast.117), calls=%async_computation.5 | async-start | bytes 2621440 | tf_op jit(solution)/shard_map/all_to_all | solution.py:30
  287.0 0.9 copy-start.8
  294.7 5.0 collective-permute-start.2
  307.3 40.4 %all-to-all-start.7 = ((f32[64,40,112]{2,1,0:T(8,128)}), f32[64,40,112]{2,1,0:T(8,128)}, u32[]{:S(2)}, u32[]{:S(2)}) async-start(f32[64,40,112]{2,1,0:T(8,128)} %bitcast.118), calls=%async_computation.7 | async-start | bytes 2621440 | tf_op jit(solution)/shard_map/all_to_all | solution.py:30
  376.1 0.9 copy-start.9
  383.9 4.9 collective-permute-start.3
  396.3 40.4 %all-to-all-start.9 = ((f32[64,40,112]{2,1,0:T(8,128)}), f32[64,40,112]{2,1,0:T(8,128)}, u32[]{:S(2)}, u32[]{:S(2)}) async-start(f32[64,40,112]{2,1,0:T(8,128)} %bitcast.119), calls=%async_computation.9 | async-start | bytes 2621440 | tf_op jit(solution)/shard_map/all_to_all | solution.py:30
  464.8 0.9 copy-start.10
  472.5 4.7 collective-permute-start.4
  484.8 40.4 %all-to-all-start.11 = ((f32[64,40,112]{2,1,0:T(8,128)}), f32[64,40,112]{2,1,0:T(8,128)}, u32[]{:S(2)}, u32[]{:S(2)}) async-start(f32[64,40,112]{2,1,0:T(8,128)} %bitcast.120), calls=%async_computation.11 | async-start | bytes 2621440 | tf_op jit(solution)/shard_map/all_to_all | solution.py:30
  526.6 7.9 %copy-start.12 = (bf16[1,7168]{1,0:T(2,128)(2,1)S(1)}, bf16[1,7168]{1,0:T(2,128)(2,1)}, u32[]{:S(2)}) copy-start(bf16[1,7168]{1,0:T(2,128)(2,1)} %param.14) | copy-start | bytes 43012
  526.7 7.9 %copy-start.13 = (s32[164]{0:T(256)S(1)}, s32[164]{0:T(256)}, u32[]{:S(2)}) copy-start(s32[164]{0:T(256)} %param.10) | copy-start | bytes 1972
  527.6 26.9 %all-to-all-start.12 = ((bf16[64,40,112]{2,1,0:T(8,128)(2,1)}), bf16[64,40,112]{2,1,0:T(8,128)(2,1)}, u32[]{:S(2)}, u32[]{:S(2)}) async-start(bf16[64,40,112]{2,1,0:T(8,128)(2,1)} %broadcast_in_dim.39), calls=%async_computation.12 | async-start | bytes 1310720 | tf_op jit(solution)/shard_map/all_to_all | solution.py:16
  562.5 4.7 collective-permute-start.5
  572.5 7.0 %copy-start.2 = (f32[40,7168]{1,0:T(8,128)S(1)}, f32[40,7168]{1,0:T(8,128)}, u32[]{:S(2)}) copy-start(f32[40,7168]{1,0:T(8,128)} %reshape.174) | copy-start | bytes 3440644
  572.5 40.5 %all-to-all-start.13 = ((f32[64,40,112]{2,1,0:T(8,128)}), f32[64,40,112]{2,1,0:T(8,128)}, u32[]{:S(2)}, u32[]{:S(2)}) async-start(f32[64,40,112]{2,1,0:T(8,128)} %bitcast.114), calls=%async_computation.13 | async-start | bytes 2621440 | tf_op jit(solution)/shard_map/all_to_all | solution.py:30
  579.5 9.3 %copy-start = (bf16[7168,1024]{1,0:T(8,128)(2,1)S(1)}, bf16[7168,1024]{1,0:T(8,128)(2,1)}, u32[]{:S(2)}) copy-start(bf16[7168,1024]{1,0:T(8,128)(2,1)} %all-gather.2.cloned.1.call-done) | copy-start | bytes 44040196
  579.5 9.6 %copy-start.3 = (f32[40,7168]{1,0:T(8,128)S(1)}, f32[40,7168]{1,0:T(8,128)}, u32[]{:S(2)}) copy-start(f32[40,7168]{1,0:T(8,128)} %reshape.177) | copy-start | bytes 3440644
  589.1 3.5 copy-start.5
  592.6 2.9 copy-start.6
  595.5 3.1 copy-start.4
  614.4 7.5 %copy-start.7 = (f32[40,7168]{1,0:T(8,128)S(1)}, f32[40,7168]{1,0:T(8,128)}, u32[]{:S(2)}) copy-start(f32[40,7168]{1,0:T(8,128)} %reshape.181) | copy-start | bytes 3440644
  615.4 26.7 %all-to-all-start.14 = ((bf16[64,40,112]{2,1,0:T(8,128)(2,1)}), bf16[64,40,112]{2,1,0:T(8,128)(2,1)S(1)}, u32[]{:S(2)}, u32[]{:S(2)}) async-start(bf16[64,40,112]{2,1,0:T(8,128)(2,1)} %broadcast_in_dim.40), calls=%async_computation.14 | async-start | bytes 1310720 | tf_op jit(solution)/shard_map/all_to_all | solution.py:16
Sparse Core Ops, SparseCore 0:
  180.1 140.4 all-gather.1
where the time goes:
time: 692 us; the launch traced here: 681 us
  waiting for transfers between devices  292 us (42%)
  starting transfers between devices  109 us (16%)
  blocking collectives  96.5 us (14%)
  local copies, waits for them, and re-layouts  80.5 us (12%)
  matrix products  51.7 us (7%)
  other arithmetic  36 us (5%)
  between operations  14.7 us (2%)
    all_to_all x7, waiting for transfers between devices, summed_on_arrival(): lax.all_to_all(cut_along(shard, dim, count), axis, 0, 0, tiled=True)  211 us
    all_to_all x4, blocking collectives, copy_for_each(): return lax.all_to_all(copies, axis, split_axis=0, concat_axis=0, tiled=True)  96.5 us
    all_to_all x5, waiting for transfers between devices, copy_for_each(): return lax.all_to_all(copies, axis, split_axis=0, concat_axis=0, tiled=True)  77.8 us
    all_to_all x7, starting transfers between devices, summed_on_arrival(): lax.all_to_all(cut_along(shard, dim, count), axis, 0, 0, tiled=True)  46.4 us
    reshape x14, local copies, waits for them, and re-layouts, cut_along(): return jnp.moveaxis(shard.reshape(*before, count, -1, *after), dim, 0)  41.1 us
    all_to_all x5, starting transfers between devices, copy_for_each(): return lax.all_to_all(copies, axis, split_axis=0, concat_axis=0, tiled=True)  39.3 us
    dot_general x7, matrix products, per_device(): logits = jnp.dot(head_input, whole_head, preferred_element_type=jnp.float32)  35.6 us
    convert_element_type x14, local copies, waits for them, and re-layouts, per_device(): rows_float = full_rows.astype(jnp.float32)  28.4 us
  transfers between devices with their start and end apart: 19, of which 18 were waited for; matrix products, arithmetic and copies ran while one was open for 17% of the time, Pallas kernels for 0%

commit v1 on v0

v1 whole, which is shorter than its diff:
```python
import functools

import jax
import jax.numpy as jnp
from jax import lax
from jax.experimental import pallas as pl
from jax.experimental.pallas import tpu as pltpu
from jax.sharding import PartitionSpec as P

EPSILON = 1e-06
NG = 8
LANES = 128
BF = jnp.bfloat16
F32 = jnp.float32
HI = lax.Precision.HIGHEST


def nt_dot(a, b):
    return lax.dot_general(a, b, (((1,), (1,)), ((), ())), precision=HI, preferred_element_type=F32)


def iota2(shape, dim):
    return lax.broadcasted_iota(jnp.int32, shape, dim)


def kernel(
    dims,
    trunk, embeds, tokens, w_hbm, hgain, egain, ogain, head_hbm,
    losses,
    te, gp, gall, eall, ssx, rms, wr, wx, headv, aown, apart, xs, xr, og0, og0r, hi0, z0, x0, ogs, oga, acc,
    psend, esend, sssend, pr, er, ssr, hown, hch, hs, zk, hx, lps, lpr, lqs, lqr,
    stats, srow, sz, fin,
    gp_ss, gp_rs, ea_ss, ea_rs, sx_ss, sx_rs, rm_ss, rm_rs, w_ss, w_rs, w_ls,
    wx_ss, wx_rs, wx_ls, ap_ss, ap_rs, xr_ss, xr_rs, hd_s, z0_ss, z0_rs, x0_ss, x0_rs,
    og_ss, og_rs, og0_ss, og0_rs, p_ss, p_rs, e_ss, e_rs, q_ss, q_rs,
    hc_ss, hc_rs, rl_ss, rl_rs, zk_ss, zk_rs, hx_ss, hx_rs, lp_ss, lp_rs,
    sr_ss, sr_rs, sz_ss, sz_rs, fin_ss, fin_rs,
):
    S, NZ, TOK, D, PW, VW = dims
    CH = NG * PW
    NT = CH // LANES
    ZS = NZ // S
    KS = D // S
    NW = D // NG
    RB = TOK // S
    s = lax.axis_index("segment")
    v = lax.axis_index("vocab")
    z = v // NG
    g = v % NG
    last = s == S - 1
    in_slice = z // ZS == s
    has = g < NT
    is_self = last & (g // ZS == S - 1) & (z == g) & has
    b_own = z % ZS
    x = g // 2
    core = g % 2
    NX = NG // 2

    def loop(n, fn, lo=0):
        def step(i, c):
            fn(i)
            return c
        lax.fori_loop(lo, n, step, 0)

    def rc(src, dst, ss, rs, dev):
        return pltpu.make_async_remote_copy(
            src_ref=src, dst_ref=dst, send_sem=ss, recv_sem=rs,
            device_id=dev, device_id_type=pl.DeviceIdType.MESH,
        )

    def row_dev(k):
        return (s, z * NG + (g + k) % NG)

    def z_dev(k):
        return (s, ((z + k) % NZ) * NG + g)

    def y_dev(k):
        return ((s + k) % S, v)

    here = (s, v)
    barrier = pltpu.get_barrier_semaphore()

    def greet(dev):
        pl.semaphore_signal(barrier, inc=1, device_id=dev, device_id_type=pl.DeviceIdType.MESH)

    loop(NG, lambda k: greet(row_dev(k)), 1)
    loop(NZ, lambda k: greet(z_dev(k)), 1)
    loop(S, lambda k: greet(y_dev(k)), 1)

    @pl.when((s >= 2) & has)
    def _():
        loop(NZ, lambda i: greet((s - 1, i * NG + z)))

    @pl.when(in_slice & has)
    def _():
        def one(i):
            @pl.when(jnp.logical_not(is_self & (i == z)))
            def _():
                greet((S - 1, i * NG + z))
        loop(NZ, one)

    owners = jnp.where(s >= 1, NT, 0) - is_self.astype(jnp.int32)
    pl.semaphore_wait(barrier, NG - 1 + NZ - 1 + S - 1 + owners)

    lane0 = (iota2((8, LANES), 1) == 0).astype(F32)
    eye = (iota2((TOK, TOK), 0) == iota2((TOK, TOK), 1)).astype(F32)

    def to_row(col):
        return nt_dot(lane0, jnp.broadcast_to(col, (TOK, LANES)))

    def to_col(row):
        return nt_dot(eye, jnp.broadcast_to(row[0:1], (LANES, TOK)))

    te[0] = trunk[...].astype(F32)
    rows = embeds[...].astype(F32)
    value = rows[0:TOK]
    for i in range(1, S):
        value = jnp.where(s == i, rows[i:i + TOK], value)
    te[1] = value
    for i, gains in enumerate((hgain, egain)):
        every = gains[...].astype(F32)
        value = every[0:1]
        for n in range(1, S - 1):
            value = jnp.where(s == n + 1, every[n:n + 1], value)
        gp[i] = jnp.broadcast_to(value, (8, PW))
    for i in range(2):
        f = te[i]
        ssx[g, i] = to_row(jnp.sum(f * f, axis=1, keepdims=True))

    def sx_copy(k, slot):
        return rc(ssx.at[g], ssx.at[slot], sx_ss.at[k], sx_rs.at[slot], row_dev(k))

    loop(NG, lambda k: sx_copy(k, g).start(), 1)

    def gp_copy(k, slot):
        return rc(gp, gall.at[slot], gp_ss.at[k], gp_rs.at[slot], row_dev(k))

    def ea_copy(k, slot):
        return rc(aown.at[1], eall.at[slot], ea_ss.at[k], ea_rs.at[slot], row_dev(k))

    def columns(n):
        return pl.ds(pl.multiple_of(n * NW, LANES), NW)

    def w_copy(h, k, slot):
        return rc(
            w_hbm.at[0, h, :, columns((g + k) % NG)],
            wr.at[h, pl.ds(pl.multiple_of(slot * PW, 16), PW), :],
            w_ss.at[h, k], w_rs.at[h, slot], row_dev(k),
        )

    def w_local(h):
        return pltpu.make_async_copy(
            w_hbm.at[0, h, :, columns(g)],
            wr.at[h, pl.ds(pl.multiple_of(g * PW, 16), PW), :],
            w_ls.at[h],
        )

    def w_start(h):
        w_local(h).start()
        loop(NG, lambda k: w_copy(h, k, g).start(), 1)

    def w_wait(h):
        w_local(h).wait()
        loop(NG, lambda k: w_copy(h, k, (g + k) % NG).wait_recv(), 1)

    partner = (s, z * NG + g + 1 - 2 * core)

    def wx_copy(h, n):
        return rc(
            w_hbm.at[0, h, :, columns(2 * n + 1 - core)],
            wx.at[pl.ds((2 + h) * PW, PW), columns(n)],
            wx_ss.at[h, n], wx_rs.at[h, n], partner,
        )

    def wx_local(h, n):
        return pltpu.make_async_copy(
            w_hbm.at[0, h, :, columns(2 * n + core)],
            wx.at[pl.ds(h * PW, PW), columns(n)],
            wx_ls.at[h, n],
        )

    @pl.when(s == 1)
    def _():
        for h in (0, 1):
            loop(NX, lambda n: wx_copy(h, n).start())
            loop(NX, lambda n: wx_local(h, n).start())

    @pl.when(s >= 2)
    def _():
        aown[1] = te[1].astype(BF)
        eall[g] = te[1].astype(BF)
        gall[g] = gp[...]
        loop(NG, lambda k: gp_copy(k, g).start(), 1)
        loop(NG, lambda k: ea_copy(k, g).start(), 1)
        w_start(1)

    head_copy = pltpu.make_async_copy(head_hbm, headv, hd_s)
    head_copy.start()

    for i in range(S):
        ogs[i] = jnp.broadcast_to(ogain[:, i * KS:(i + 1) * KS].astype(F32), (8, KS))

    def og_copy(k, slot):
        return rc(ogs.at[(s + k) % S], oga.at[slot], og_ss.at[k], og_rs.at[slot], y_dev(k))

    loop(S, lambda k: og_copy(k, s).start(), 1)
    oga[s] = ogs[s]

    def og0_copy(k):
        return rc(og0, og0r, og0_ss.at[k], og0_rs, y_dev(k))

    @pl.when(s == 0)
    def _():
        chunk = jnp.broadcast_to(ogain[:, pl.ds(pl.multiple_of(z * CH, LANES), CH)].astype(F32), (8, CH))
        spot = iota2((CH, PW), 0) == iota2((CH, PW), 1) + g * PW
        og0[...] = jnp.dot(chunk.astype(BF), spot.astype(BF), preferred_element_type=F32)
        og0r[...] = og0[...]
        loop(S, lambda k: og0_copy(k).start(), 1)

    loop(NG, lambda k: sx_copy(k, (g + k) % NG).wait_recv(), 1)
    value = ssx[0]
    for i in range(1, NG):
        value = value + ssx[i]
    rms[z] = value

    def rm_copy(k, slot):
        return rc(rms.at[z], rms.at[slot], rm_ss.at[k], rm_rs.at[slot], z_dev(k))

    loop(NZ, lambda k: rm_copy(k, z).start(), 1)
    loop(NZ, lambda k: rm_copy(k, (z + k) % NZ).wait_recv(), 1)
    value = rms[0]
    for i in range(1, NZ):
        value = value + rms[i]
    value = lax.rsqrt(value / D + EPSILON)
    trunk_scale = to_col(value[0])[:, :1]
    embed_scale = to_col(value[1])[:, :1]

    role = last.astype(jnp.int32)
    dplane = jnp.where(last, g // ZS, s + 1)

    def p_copy(j):
        return rc(psend.at[j], pr.at[role, z], p_ss.at[j], p_rs.at[role, z], (dplane, g * NG + j))

    def q_copy(j):
        return rc(sssend, ssr.at[role, z], q_ss.at[j], q_rs.at[role, z], (dplane, g * NG + j))

    def e_copy(j):
        return rc(esend.at[j], er.at[role, z], e_ss.at[j], e_rs.at[role, z], (dplane, g * NG + j))

    def each_owner(away, own):
        def one(j):
            mine = is_self & (j == g)

            @pl.when(jnp.logical_not(mine))
            def _():
                away(j)

            if own is not None:
                @pl.when(mine)
                def _():
                    own(j)
        loop(NT, one)

    def e_send():
        def own(j):
            er[1, z] = esend[j]
        each_owner(lambda j: e_copy(j).start(), own)

    def ap_copy():
        return rc(aown, apart, ap_ss, ap_rs, partner)

    def xr_copy(n, slot):
        return rc(xs.at[n], xr.at[slot], xr_ss.at[n], xr_rs.at[slot], (s, z * NG + 2 * n + core))

    @pl.when(s == 1)
    def _():
        aown[0] = (te[0] * trunk_scale * gp[0, 0:1]).astype(BF)
        aown[1] = (te[1] * embed_scale * gp[1, 0:1]).astype(BF)
        ap_copy().start()
        for h in (0, 1):
            def landed(n):
                wx_local(h, n).wait()
                wx_copy(h, n).wait_recv()
            loop(NX, landed)
        ap_copy().wait_recv()

        def one(i):
            n = (x + i) % NX
            total = jnp.zeros((TOK, NW), F32)
            for h in (0, 1):
                total = total + jnp.dot(aown[h], wx[h * PW:(h + 1) * PW, columns(n)], preferred_element_type=F32)
                total = total + jnp.dot(apart[h], wx[(2 + h) * PW:(3 + h) * PW, columns(n)], preferred_element_type=F32)

            @pl.when(n != x)
            def _():
                xs[n] = total.astype(BF)
                xr_copy(n, x).start()

            @pl.when(n == x)
            def _():
                acc[:, :NW] = total
        loop(NX + 1, one, 1)

        def add(i):
            n = (x + i) % NX
            xr_copy(0, n).wait_recv()
            acc[:, :NW] += xr[n].astype(F32)
        loop(NX, add, 1)
        for j in range(NT):
            esend[j] = acc[:, j * LANES:(j + 1) * LANES]
        e_send()

    @pl.when(s != 0)
    def _():
        og0_copy(0).wait_recv()

    def z0_copy(k, b):
        return rc(hi0, z0.at[b], z0_ss.at[k], z0_rs.at[b], z_dev(k))

    @pl.when(in_slice)
    def _():
        hi0[...] = (te[0] * trunk_scale * og0r[0:1]).astype(BF)
        z0[b_own] = hi0[...]
        loop(NZ, lambda k: z0_copy(k, b_own).start(), 1)

    def x0_copy(k, b, slot):
        return rc(z0.at[b], x0.at[b * NG + slot], x0_ss.at[b, k], x0_rs.at[b, slot], row_dev(k))

    for b in range(ZS):
        @pl.when(z != s * ZS + b)
        def _():
            z0_copy(0, b).wait_recv()
        loop(NG, lambda k: x0_copy(k, b, g).start(), 1)
        x0[b * NG + g] = z0[b]

    @pl.when(s >= 2)
    def _():
        w_start(0)
        loop(NG, lambda k: gp_copy(k, (g + k) % NG).wait_recv(), 1)
        loop(NG, lambda k: ea_copy(k, (g + k) % NG).wait_recv(), 1)
        acc[:, :NW] = jnp.zeros((TOK, NW), F32)
        w_wait(1)

        def one(i):
            a = (eall[i].astype(F32) * embed_scale * gall[i, 1][0:1]).astype(BF)
            rows = wr[1, pl.ds(pl.multiple_of(i * PW, 16), PW), :]
            acc[:, :NW] += jnp.dot(a, rows, preferred_element_type=F32)
        loop(NG, one)
        for j in range(NT):
            esend[j] = acc[:, j * LANES:(j + 1) * LANES]
        e_send()

    def lp_copy(k, i, slot):
        if k == S - 1:
            return rc(lps.at[(s + i) % S], lpr.at[slot], lp_ss.at[k, i], lp_rs.at[k, slot], y_dev(i))
        return rc(lqs.at[k, (s + i) % S], lqr.at[k, slot], lp_ss.at[k, i], lp_rs.at[k, slot], y_dev(i))

    def head_send(k, total, col):
        lane = iota2((TOK, LANES), 1)
        if col is None:
            tail = jnp.zeros((TOK, LANES), F32)
        elif k < S - 1:
            tail = jnp.where(lane == 0, col, 0.0)
        else:
            hi = col.astype(BF).astype(F32)
            mid = (col - hi).astype(BF).astype(F32)
            low = col - hi - mid
            tail = jnp.where(lane == 0, hi, jnp.where(lane == 1, mid, jnp.where(lane == 2, low, 0.0)))
        for i in range(S):
            rows = slice(i * RB, (i + 1) * RB)
            if k == S - 1:
                lps[i, :, :VW] = total[rows].astype(BF)
                lps[i, :, VW:] = tail[rows].astype(BF)
            else:
                lqs[k, i, :, :VW] = total[rows]
                lqs[k, i, :, VW:] = tail[rows]
        loop(S, lambda i: lp_copy(k, i, s).start(), 1)
        if k == S - 1:
            lpr[s] = lps[s]
        else:
            lqr[k, s] = lqs[k, s]

    def head_lse(k):
        loop(S, lambda i: lp_copy(k, i, (s + i) % S).wait_recv(), 1)
        parts = [(lpr[i] if k == S - 1 else lqr[k, i]).astype(F32) for i in range(S)]
        total = parts[0]
        for part in parts[1:]:
            total = total + part
        logits = total[:, :VW]
        if k > 0:
            logits = logits * lax.rsqrt(jnp.sum(total[:, VW:], axis=1, keepdims=True) / D + EPSILON)
        top = jnp.max(logits, axis=1, keepdims=True)
        summed = jnp.sum(jnp.exp(logits - top), axis=1, keepdims=True)
        target = tokens[pl.ds(s * RB + k + 1, RB), :] - v * VW
        pick = jnp.sum(jnp.where(iota2((RB, VW), 1) == target, logits, 0.0), axis=1, keepdims=True)
        lane = iota2((RB, LANES), 1)
        stats[k * RB:(k + 1) * RB, :] = jnp.where(
            lane == 0, top, jnp.where(lane == 1, summed, jnp.where(lane == 2, pick, 0.0)))

    def head0():
        for b in range(ZS):
            loop(NG, lambda k: x0_copy(k, b, (g + k) % NG).wait_recv(), 1)
        acc[:, :VW] = jnp.zeros((TOK, VW), F32)

        def one(i):
            rows = headv[pl.ds(pl.multiple_of(i * PW, 16), PW), :]
            acc[:, :VW] += jnp.dot(x0[i], rows, preferred_element_type=F32)
        loop(ZS * NG, one)
        head_send(0, acc[:, :VW], None)

    def owner(r, k):
        def one(i):
            def waits():
                rc(esend.at[0], er.at[r, i], e_ss.at[0], e_rs.at[r, i], here).wait_recv()

            if r == 0:
                waits()
            else:
                pl.when(jnp.logical_not(is_self & (i == z)))(waits)
        loop(NZ, one)
        total = er[r, 0]
        for i in range(1, NZ):
            total = total + er[r, i]
        if k > 1:
            def one(i):
                def waits():
                    rc(psend.at[0], pr.at[r, i], p_ss.at[0], p_rs.at[r, i], here).wait_recv()
                    rc(sssend, ssr.at[r, i], q_ss.at[0], q_rs.at[r, i], here).wait_recv()

                if r == 0:
                    waits()
                else:
                    pl.when(jnp.logical_not(is_self & (i == z)))(waits)
            loop(NZ, one)
            part = pr[r, 0].astype(F32)
            ss = ssr[r, 0]
            for i in range(1, NZ):
                part = part + pr[r, i].astype(F32)
                ss = ss + ssr[r, i]
            total = part * to_col(lax.rsqrt(ss / D + EPSILON)) + total
        return total.astype(BF)

    def hc_copy(k, slot):
        return rc(hown, hch.at[:, pl.ds(pl.multiple_of(slot * LANES, LANES), LANES)],
                  hc_ss.at[k], hc_rs.at[slot], row_dev(k))

    def rl_copy(k):
        return rc(hown, hs.at[k], rl_ss, rl_rs.at[k], (z // ZS, v))

    def chain(k):
        @pl.when((s == k + 1) & has)
        def _():
            h = owner(0, k)
            hown[...] = h
            loop(NG, lambda i: hc_copy(i, g).start(), 1)

            @pl.when(jnp.logical_not(in_slice))
            def _():
                rl_copy(k).start()

            @pl.when(in_slice)
            def _():
                hs[k] = h
            hch[:, pl.ds(pl.multiple_of(g * LANES, LANES), LANES)] = h

        @pl.when(s == k + 1)
        def _():
            def one(i):
                @pl.when(i != g)
                def _():
                    hc_copy(0, i).wait_recv()
            loop(NT, one)
            w_wait(0)
            f = hch[...].astype(F32)
            gain = jnp.zeros((8, CH), F32)
            for i in range(NG):
                spot = iota2((PW, CH), 0) + i * PW == iota2((PW, CH), 1)
                gain = gain + jnp.dot(gall[i, 0].astype(BF), spot.astype(BF), preferred_element_type=F32)
            a = (f * gain[0:1]).astype(BF)
            total = jnp.dot(a, wr[0], preferred_element_type=F32)
            for j in range(NT):
                psend[j] = total[:, j * LANES:(j + 1) * LANES].astype(BF)
            sssend[...] = to_row(jnp.sum(f * f, axis=1, keepdims=True))

            def away(j):
                p_copy(j).start()
                q_copy(j).start()

            def own(j):
                pr[1, z] = psend[j]
                ssr[1, z] = sssend[...]
            each_owner(away, own)

    def zk_copy(k, i, b):
        return rc(hs.at[k], zk.at[k, b], zk_ss.at[k, i], zk_rs.at[k, b], z_dev(i))

    def spread(k):
        @pl.when(in_slice & has)
        def _():
            if k < S - 1:
                @pl.when(s != k + 1)
                def _():
                    rl_copy(k).wait_recv()
            loop(NZ, lambda i: zk_copy(k, i, b_own).start(), 1)
            zk[k, b_own] = hs[k]

    def hx_at(k, b, slot):
        return hx.at[k, :, pl.ds(pl.multiple_of(b * CH + slot * LANES, LANES), LANES)]

    def hx_copy(k, b, i, slot):
        return rc(zk.at[k, b], hx_at(k, b, slot), hx_ss.at[k, b, i], hx_rs.at[k, b, slot], row_dev(i))

    def gather(k):
        @pl.when(has)
        def _():
            for b in range(ZS):
                @pl.when(z != s * ZS + b)
                def _():
                    zk_copy(k, 0, b).wait_recv()
                loop(NG, lambda i: hx_copy(k, b, i, g).start(), 1)
                hx[k, :, pl.ds(pl.multiple_of(b * CH + g * LANES, LANES), LANES)] = zk[k, b]

    def head(k):
        for b in range(ZS):
            def one(i):
                @pl.when(i != g)
                def _():
                    hx_copy(k, b, 0, i).wait_recv()
            loop(NT, one)
        f = hx[k].astype(F32)
        a = (f * oga[k][0:1]).astype(BF)
        total = jnp.dot(a, headv[...], preferred_element_type=F32)
        head_send(k, total, jnp.sum(f * f, axis=1, keepdims=True))

    loop(S, lambda k: og_copy(k, (s + k) % S).wait_recv(), 1)
    for k in range(1, S - 1):
        chain(k)
        spread(k)
        if k == 1:
            head_copy.wait()
            head0()
        else:
            head(k - 1)
        if k < S - 2:
            gather(k)
    head_lse(0)
    gather(S - 2)

    @pl.when(in_slice & has)
    def _():
        hs[S - 1] = owner(1, S - 1)
    spread(S - 1)
    head(S - 2)
    for k in range(1, S - 2):
        head_lse(k)
    gather(S - 1)
    head_lse(S - 2)
    head(S - 1)
    head_lse(S - 1)

    pick_row = (iota2((8, LANES), 0) == iota2((8, LANES), 1)).astype(F32)
    srow[g] = nt_dot(pick_row, stats[...])

    def merged(ref, n):
        top = ref[0, 0:1]
        for i in range(1, n):
            top = jnp.maximum(top, ref[i, 0:1])
        summed = jnp.zeros((1, TOK), F32)
        pick = jnp.zeros((1, TOK), F32)
        for i in range(n):
            summed = summed + ref[i, 1:2] * jnp.exp(ref[i, 0:1] - top)
            pick = pick + ref[i, 2:3]
        return top, summed, pick

    def sr_copy(k, slot):
        return rc(srow.at[g], srow.at[slot], sr_ss.at[k], sr_rs.at[slot], row_dev(k))

    loop(NG, lambda k: sr_copy(k, g).start(), 1)
    loop(NG, lambda k: sr_copy(k, (g + k) % NG).wait_recv(), 1)
    top, summed, pick = merged(srow, NG)
    line = iota2((8, TOK), 0)
    sz[z] = jnp.where(line == 0, top, jnp.where(line == 1, summed, pick))

    def sz_copy(k, slot):
        return rc(sz.at[z], sz.at[slot], sz_ss.at[k], sz_rs.at[slot], z_dev(k))

    loop(NZ, lambda k: sz_copy(k, z).start(), 1)
    loop(NZ, lambda k: sz_copy(k, (z + k) % NZ).wait_recv(), 1)
    top, summed, pick = merged(sz, NZ)
    fin[s] = jnp.broadcast_to(top + jnp.log(summed) - pick, (8, TOK))

    def fin_copy(k, slot):
        return rc(fin.at[s], fin.at[slot], fin_ss.at[k], fin_rs.at[slot], y_dev(k))

    loop(S, lambda k: fin_copy(k, s).start(), 1)
    loop(S, lambda k: fin_copy(k, (s + k) % S).wait_recv(), 1)
    value = jnp.zeros((8, TOK), F32)
    for i in range(S):
        row, col = iota2((TOK, TOK), 0), iota2((TOK, TOK), 1)
        spot = (row - s * RB == col - i * RB) & (col >= i * RB) & (col < (i + 1) * RB)
        value = value + jnp.dot(fin[i], spot.astype(F32), precision=HI, preferred_element_type=F32)
    losses[...] = value[0:1]

    loop(NG, lambda k: sx_copy(k, g).wait_send(), 1)
    loop(NZ, lambda k: rm_copy(k, z).wait_send(), 1)
    loop(S, lambda k: og_copy(k, s).wait_send(), 1)

    @pl.when(s == 0)
    def _():
        loop(S, lambda k: og0_copy(k).wait_send(), 1)

    @pl.when(in_slice)
    def _():
        loop(NZ, lambda k: z0_copy(k, b_own).wait_send(), 1)

    @pl.when(s >= 1)
    def _():
        each_owner(lambda j: e_copy(j).wait_send(), None)

    @pl.when(s == 1)
    def _():
        ap_copy().wait_send()
        for h in (0, 1):
            loop(NX, lambda n: wx_copy(h, n).wait_send())
        loop(NX, lambda i: xr_copy((x + i) % NX, x).wait_send(), 1)

    @pl.when(s >= 2)
    def _():
        loop(NG, lambda k: gp_copy(k, g).wait_send(), 1)
        loop(NG, lambda k: ea_copy(k, g).wait_send(), 1)
        for h in (1, 0):
            loop(NG, lambda k: w_copy(h, k, g).wait_send(), 1)

        def sent(j):
            p_copy(j).wait_send()
            q_copy(j).wait_send()
        each_owner(sent, None)

    for b in range(ZS):
        loop(NG, lambda k: x0_copy(k, b, g).wait_send(), 1)

    @pl.when((s >= 2) & has)
    def _():
        loop(NG, lambda i: hc_copy(i, g).wait_send(), 1)

        @pl.when(jnp.logical_not(in_slice))
        def _():
            rl_copy(0).wait_send()

    for k in range(1, S):
        @pl.when(in_slice & has)
        def _():
            loop(NZ, lambda i: zk_copy(k, i, b_own).wait_send(), 1)

        @pl.when(has)
        def _():
            for b in range(ZS):
                loop(NG, lambda i: hx_copy(k, b, i, g).wait_send(), 1)
    for k in range(S):
        loop(S, lambda i: lp_copy(k, i, s).wait_send(), 1)
    loop(NG, lambda k: sr_copy(k, g).wait_send(), 1)
    loop(NZ, lambda k: sz_copy(k, z).wait_send(), 1)
    loop(S, lambda k: fin_copy(k, s).wait_send(), 1)


def per_device(
    trunk_out, embeds, token_ids, module_weight, hidden_gain, embed_gain, out_gain, head_weight
):
    S = lax.axis_size("segment")
    V = lax.axis_size("vocab")
    TOK, PW = trunk_out.shape
    D = PW * V
    NZ = V // NG
    VW = head_weight.shape[1]
    CH = NG * PW
    NT = CH // LANES
    ZS = NZ // S
    KS = D // S
    NW = D // NG
    RB = TOK // S
    assert NZ == NG and KS == head_weight.shape[0]
    vm = pl.BlockSpec(memory_space=pltpu.VMEM)
    hbm = pl.BlockSpec(memory_space=pl.ANY)
    dma = pltpu.SemaphoreType.DMA
    ACC = max(VW, NW)
    scratch = [
        pltpu.VMEM((2, TOK, PW), F32),
        pltpu.VMEM((2, 8, PW), F32),
        pltpu.VMEM((NG, 2, 8, PW), F32),
        pltpu.VMEM((NG, TOK, PW), BF),
        pltpu.VMEM((NG, 2, 8, TOK), F32),
        pltpu.VMEM((NZ, 2, 8, TOK), F32),
        pltpu.VMEM((2, CH, NW), BF),
        pltpu.VMEM((4 * PW, NG // 2 * NW), BF),
        pltpu.VMEM((KS, VW), BF),
        pltpu.VMEM((2, TOK, PW), BF),
        pltpu.VMEM((2, TOK, PW), BF),
        pltpu.VMEM((NG // 2, TOK, NW), BF),
        pltpu.VMEM((NG // 2, TOK, NW), BF),
        pltpu.VMEM((8, PW), F32),
        pltpu.VMEM((8, PW), F32),
        pltpu.VMEM((TOK, PW), BF),
        pltpu.VMEM((ZS, TOK, PW), BF),
        pltpu.VMEM((ZS * NG, TOK, PW), BF),
        pltpu.VMEM((S, 8, KS), F32),
        pltpu.VMEM((S, 8, KS), F32),
        pltpu.VMEM((TOK, ACC), F32),
        pltpu.VMEM((NT, TOK, LANES), BF),
        pltpu.VMEM((NT, TOK, LANES), F32),
        pltpu.VMEM((8, TOK), F32),
        pltpu.VMEM((2, NZ, TOK, LANES), BF),
        pltpu.VMEM((2, NZ, TOK, LANES), F32),
        pltpu.VMEM((2, NZ, 8, TOK), F32),
        pltpu.VMEM((TOK, LANES), BF),
        pltpu.VMEM((TOK, CH), BF),
        pltpu.VMEM((S, TOK, LANES), BF),
        pltpu.VMEM((S, ZS, TOK, LANES), BF),
        pltpu.VMEM((S, TOK, KS), BF),
        pltpu.VMEM((S, RB, VW + LANES), BF),
        pltpu.VMEM((S, RB, VW + LANES), BF),
        pltpu.VMEM((S - 1, S, RB, VW + LANES), F32),
        pltpu.VMEM((S - 1, S, RB, VW + LANES), F32),
        pltpu.VMEM((TOK, LANES), F32),
        pltpu.VMEM((NG, 8, TOK), F32),
        pltpu.VMEM((NZ, 8, TOK), F32),
        pltpu.VMEM((S, 8, TOK), F32),
        dma((NG,)), dma((NG,)), dma((NG,)), dma((NG,)), dma((NZ,)), dma((NZ,)),
        dma((NG,)), dma((NG,)), dma((2, NG)), dma((2, NG)), dma((2,)),
        dma((2, NG // 2)), dma((2, NG // 2)), dma((2, NG // 2)), dma(()), dma(()),
        dma((NG // 2,)), dma((NG // 2,)), dma(()),
        dma((NZ,)), dma((ZS,)),
        dma((ZS, NG)), dma((ZS, NG)),
        dma((S,)), dma((S,)), dma((S,)), dma(()),
        dma((NT,)), dma((2, NZ)), dma((NT,)), dma((2, NZ)), dma((NT,)), dma((2, NZ)),
        dma((NG,)), dma((NG,)),
        dma(()), dma((S,)),
        dma((S, NZ)), dma((S, ZS)),
        dma((S, ZS, NG)), dma((S, ZS, NG)),
        dma((S, S)), dma((S, S)),
        dma((NG,)), dma((NG,)), dma((NZ,)), dma((NZ,)), dma((S,)), dma((S,)),
    ]
    return pl.pallas_call(
        functools.partial(kernel, (S, NZ, TOK, D, PW, VW)),
        out_shape=jax.ShapeDtypeStruct((1, TOK), F32),
        in_specs=[vm, vm, vm, hbm, vm, vm, vm, hbm],
        out_specs=vm,
        scratch_shapes=scratch,
        compiler_params=pltpu.CompilerParams(collective_id=0, has_side_effects=True),
    )(trunk_out, embeds, token_ids[:, None], module_weight, hidden_gain, embed_gain, out_gain, head_weight)


def solution(mesh):
    in_specs = (
        P(None, "vocab"),
        P(None, "vocab"),
        P(),
        P("segment", None, "vocab", None),
        P(None, "vocab"),
        P(None, "vocab"),
        P("segment", None),
        P("segment", "vocab"),
    )
    return jax.shard_map(
        per_device, mesh=mesh, in_specs=in_specs, out_specs=P("segment", None), check_vma=False
    )
```

time: 692 us -> 198 us (0.29); the launches traced: 681 us -> 198 us
  waiting for transfers between devices: 292 us -> 0 us
  Pallas kernels: 0 us -> 196 us
  starting transfers between devices: 109 us -> 0 us
  blocking collectives: 96.5 us -> 0 us
  local copies, waits for them, and re-layouts: 80.5 us -> 2.64 us
  matrix products: 51.7 us -> 0 us
  other arithmetic: 36 us -> 0 us
  between operations: 14.7 us -> 0.01 us
    all_to_all x12 -> x0, waiting for transfers between devices: 289 us -> none  [the longest x7 211 us: summed_on_arrival(): lax.all_to_all(cut_along(shard, dim, count), axis, 0, 0, tiled=True)]
    pallas_call x0 -> x1, Pallas kernels: none -> 196 us  [per_device(): pl.pallas_call(functools.partial(kernel, (S, NZ, TOK, D, PW, VW)), out_sh...]
    all_to_all x4 -> x0, blocking collectives: 96.5 us -> none  [copy_for_each(): return lax.all_to_all(copies, axis, split_axis=0, concat_axis=0, tiled=True)]
    all_to_all x12 -> x0, starting transfers between devices: 85.7 us -> none  [the longest x7 46.4 us: summed_on_arrival(): lax.all_to_all(cut_along(shard, dim, count), axis, 0, 0, tiled=True)]
    dot_general x21 -> x0, matrix products: 51.7 us -> none  [the longest x7 35.6 us: per_device(): logits = jnp.dot(head_input, whole_head, preferred_element_type=jnp.float32)]
    reshape x14 -> x0, local copies, waits for them, and re-layouts: 41.1 us -> none  [cut_along(): return jnp.moveaxis(shard.reshape(*before, count, -1, *after), dim, 0)]
    convert_element_type x14 -> x0, local copies, waits for them, and re-layouts: 28.4 us -> none  [per_device(): rows_float = full_rows.astype(jnp.float32)]
    ppermute x6 -> x0, starting transfers between devices: 23.1 us -> none  [passed_along(): return lax.ppermute(block, axis, route)]
  transfers between devices with their start and end apart: 19 -> 0, of which waited for: 18 -> 0; matrix products, arithmetic and copies ran while one was open for 17% -> 0% of each run, Pallas kernels for 0% -> 0%
where the time goes in v1:
time: 198 us
  Pallas kernels  196 us (99%)
  local copies, waits for them, and re-layouts  2.64 us (1%)
    pallas_call x1, Pallas kernels, per_device(): pl.pallas_call(functools.partial(kernel, (S, NZ, TOK, D, PW, VW)), out_sh...  196 us

profile of v1, /device:TPU:1, one launch (start us, length us, event | category | flops | bytes accessed | tf_op | source)
XLA Modules:
  0.0 198.3 jit_solution(5540737844868590159)
XLA Ops:
  0.0 1.4 copy.9.tokens
  1.4 195.6 %shard_map.82 = f32[1,160]{1,0:T(1,128)} custom-call(bf16[160,112]{1,0:T(8,128)(2,1)} %trunk.1, bf16[164,112]{1,0:T(8,128)(2,1)} %embeds.1, s32[164,1]{1,0:T(8,128)} %copy.9.tokens, bf16[1,2,112,7168]{3,2,1,0:T(8,128)(2,1)} %w_hbm.1, bf16[3,112]{1,0:T(4,128)(2,1)} %hgain.1, bf16[3,112]{1,0:T(4,128)(2,1)} %egain.1, bf16[1,7168]{1,0:T(2,128)(2,1)} %ogain.1, ...), custom_call_target="tpu_custom_call" | custom-call | tf_op jit(solution)/shard_map/pallas_call | solution.py:742
  197.1 1.2 copy.11
